TPU v7x, 128 devices: a whole 4x4x4 slice. The times are simulated.
128 devices in a mesh: gx: 16 (over y, z), gy: 8 (over x, core).
Axes of the slice: x: 4, y: 4, z: 4, core: 2. Of those that a mesh axis runs over, the one named last changes fastest.
Arguments:
- state: float32 [8, 2, 4194304], P('gy', None, 'gx'), may hold values from -6 to 6
- fields: float32 [22], replicated, may hold values from 0.5 to 2
- couplings: float32 [22], replicated, may hold values from 0.5 to 2
- noise: float32 [8, 4, 2], P('gy'), may hold values from -5 to 5
Outputs:
- final_state: float32 [8, 2, 4194304], P('gy', None, 'gx')
- record: float32 [4, 2], replicated
All inputs are finite; a program needn't handle non-finite values.
Results may differ from a plain program's by a relative error of at most 0.0001.
Values sent between devices are 32-bit elements; how exact they have to be, the bound alone decides.
A program may use at most 128 MiB of HBM per device.

v0:
```python
import jax
import jax.numpy as jnp
from jax import lax
from jax.sharding import PartitionSpec as P

kappa_rate = 4.0
time_step = 0.05


def from_partner(array, axis, bit):
    return lax.ppermute(array, axis, [(i, i ^ 1 << bit) for i in range(lax.axis_size(axis))])


def sent_to_all(array, axis):
    length = lax.axis_size(axis)
    return lax.all_to_all(
        jnp.broadcast_to(array[None], (length, *array.shape)), axis, 0, 0, tiled=True
    )


def taken_together(array, axis):
    return sent_to_all(array, axis).sum(axis=0)


def in_one(arrays, axis):
    line, at, finished = (jnp.concatenate([a.reshape(-1) for a in arrays]), 0, [])
    running = taken_together(line, axis)
    for a in arrays:
        finished.append(running[at : at + a.size].reshape(a.shape))
        at += a.size
    return tuple(finished)


def flip_table(fields, lowest, width):
    row_ids = lax.iota(jnp.int32, 1 << width)
    row_xor = row_ids[:, None] ^ row_ids[None, :]
    table = jnp.zeros((1 << width, 1 << width), jnp.float32)
    for q in range(width):
        table = table + fields[lowest + q] * (row_xor == 1 << q).astype(jnp.float32)
    return table


def block_flip(amplitudes, lowest, width, table):
    shape = amplitudes.shape
    if lowest == 0:
        return jnp.dot(
            amplitudes.reshape(-1, 1 << width),
            table,
            precision=lax.Precision.HIGHEST,
            preferred_element_type=jnp.float32,
        ).reshape(shape)
    viewed = amplitudes.reshape(
        shape[0], shape[1], shape[2] >> lowest + width, 1 << width, 1 << lowest
    )
    result = jnp.einsum(
        "pcakb,kj->pcajb",
        viewed,
        table,
        precision=lax.Precision.HIGHEST,
        preferred_element_type=jnp.float32,
    )
    return result.reshape(shape)


def shards(state, fields, couplings, noise):
    local_len = state.shape[2]
    low_bits = local_len.bit_length() - 1
    group_count = lax.axis_size("gx")
    high_bits = group_count.bit_length() - 1
    count_qubits = low_bits + high_bits
    position = lax.axis_index("gx") * local_len + lax.iota(jnp.int32, local_len)
    first_spin = 1.0 - 2.0 * (position & 1).astype(jnp.float32)
    prior_spin = first_spin
    occupancy = 0.5 * (1.0 - first_spin)
    energy = jnp.zeros((local_len,), jnp.float32)
    for q in range(1, count_qubits):
        spin_now = 1.0 - 2.0 * (position >> q & 1).astype(jnp.float32)
        occupancy = occupancy + 0.5 * (1.0 - spin_now)
        energy = energy + couplings[q - 1] * prior_spin * spin_now
        prior_spin = spin_now
    energy = energy + couplings[count_qubits - 1] * prior_spin * first_spin
    occupancy = occupancy / count_qubits
    block_list = []
    lowest = 0
    while lowest < low_bits:
        width = min(7, low_bits - lowest)
        block_list.append((lowest, width, flip_table(fields, lowest, width)))
        lowest = lowest + width
    amplitudes = state
    half_root = jnp.sqrt(jnp.float32(time_step / 2.0))
    root_kappa = jnp.sqrt(jnp.float32(kappa_rate))
    step_records = []
    for step_id in range(noise.shape[1]):
        result = None
        for apply_lowest, apply_width, table in block_list:
            term = block_flip(amplitudes, apply_lowest, apply_width, table)
            result = term if result is None else result + term
        for b in range(high_bits):
            result = result + fields[low_bits + b] * from_partner(amplitudes, "gx", b)
        weight = amplitudes[:, 0] ** 2 + amplitudes[:, 1] ** 2
        norm_sum, magnet_sum = in_one(
            (jnp.sum(weight, axis=1), jnp.sum(weight * occupancy[None, :], axis=1)), "gx"
        )
        magnet = magnet_sum / norm_sum
        factor = jnp.sqrt(local_len * group_count / norm_sum)[:, None]
        shift = occupancy[None, :] - magnet[:, None]
        first = (noise[:, step_id, 0] * half_root)[:, None]
        second = (noise[:, step_id, 1] * half_root)[:, None]
        real_part = amplitudes[:, 0]
        imag_part = amplitudes[:, 1]
        keep = 1.0 - time_step * kappa_rate * 0.5 * shift * shift + time_step * 0.0
        kick = root_kappa * shift
        coherent_real = -result[:, 1] - energy[None, :] * imag_part
        coherent_imag = -result[:, 0] - energy[None, :] * real_part
        new_real = factor * (
            keep * real_part
            + time_step * coherent_real
            + kick * (real_part * first - imag_part * second)
        )
        new_imag = factor * (
            keep * imag_part
            - time_step * coherent_imag
            + kick * (real_part * second + imag_part * first)
        )
        amplitudes = jnp.stack([new_real, new_imag], axis=1)
        drift = root_kappa * magnet * time_step
        local_record = jnp.sum(
            jnp.stack([drift + first[:, 0], drift + second[:, 0]], axis=1), axis=0
        )
        step_records.append(local_record)
    record = lax.psum(jnp.stack(step_records), "gy")
    return (amplitudes, record)


def solution(mesh):
    placed = (P("gy", None, "gx"), P(), P(), P("gy", None, None))
    return jax.shard_map(
        shards, mesh=mesh, in_specs=placed, out_specs=(P("gy", None, "gx"), P()), check_vma=False
    )
```

profile of v0, /device:TPU:1, one launch (start us, length us, event | category | flops | bytes accessed | tf_op | source)
XLA Modules:
  0.0 806.3 jit_solution(12119691998441880718)
XLA Ops:
  0.6 4.5 collective-permute-start.1
  9.2 46.5 %fusion.156 = (f32[]{:T(128)}, f32[]{:T(128)}) fusion(s32[]{:T(128)S(6)} %mul.5966, f32[1,2,262144]{2,1,0:T(2,128)} %param.4), kind=kLoop, calls=%fused_computation.311 | loop fusion | flops 41943040 | bytes 2097164 | tf_op jit(solution)/shard_map/reduce_sum | solution.py:102
  57.6 3.7 all-to-all-start
  61.4 3.1 reshape.2342
  69.8 6.6 convolution_bitcast_fusion.3
  76.4 4.7 reshape.2347
  81.3 7.5 convolution_bitcast_fusion.5
  88.8 4.2 reshape.2345
  95.1 9.5 %convolution_bitcast_fusion.4 = f32[4096,128]{0,1:T(8,128)} fusion(f32[4096,128]{1,0:T(8,128)} %reshape.2342, f32[]{:T(128)} %bitcast.12, f32[]{:T(128)} %bitcast.11, f32[]{:T(128)} %bitcast.10, f32[]{:T(128)} %bitcast.9, f32[]{:T(128)} %bitcast.8, f32[]{:T(128)} %bitcast.7, f32[]{:T(128)} %bitcast.6), kind=kOutput, calls=%fused_computation.4 | convolution fusion | flops 805650432 | bytes 4194332 | tf_op jit(solution)/shard_map/dot_general | solution.py:46
  107.4 4.2 reshape.2343
  114.5 9.2 %multiply_add_fusion.3 = f32[1,2,262144]{2,1,0:T(2,128)S(1)} fusion(f32[1,2,262144]{2,1,0:T(2,128)} %collective-permute-done.3, f32[1,2,262144]{2,1,0:T(2,128)} %collective-permute-done.2, f32[1,2,262144]{2,1,0:T(2,128)} %collective-permute-done.1, f32[1,2,262144]{2,1,0:T(2,128)} %collective-permute-done, f32[1,2,262144]{2,1,0:T(2,128)} %reshape.2347, ...), kind=kLoop, calls=%fused_computation.35 | loop fusion | flops 5242880 | bytes 16777232 | tf_op jit(solution)/shard_map/add | solution.py:99
  123.7 79.3 %add_multiply_fusion.10 = (f32[1,1,262144]{2,1,0:T(1,128)S(1)}, f32[1,1,262144]{2,1,0:T(1,128)S(1)}) fusion(f32[]{:T(128)} %bitcast.60, f32[]{:T(128)} %bitcast.59, f32[]{:T(128)} %bitcast.5, s32[]{:T(128)S(6)} %mul.5966, f32[]{:T(128)} %bitcast.4, f32[1,2,262144]{2,1,0:T(2,128)S(1)} %multiply_add_fusion.3, f32[1,2,262144]{2,1,0:T(2,128)S(1)} %copy-done, ...), kind=kLoop, calls=%fused_computation.103 | loop fusion | flops 61865984 | bytes 5242988 | tf_op jit(solution)/shard_map/mul | solution.py:115
  203.0 49.4 %slice_negate_fusion.7 = (f32[1,1,262144]{2,1,0:T(1,128)}, f32[1,1,262144]{2,1,0:T(1,128)S(1)}, f32[1,1,262144]{2,1,0:T(1,128)}, f32[1,1,262144]{2,1,0:T(1,128)}, f32[1,1,262144]{2,1,0:T(1,128)}) fusion(f32[1,2,262144]{2,1,0:T(2,128)S(1)} %multiply_add_fusion.3, f32[]{:T(128)} %bitcast.59, f32[]{:T(128)} %bitcast.60, ...), kind=kLoop, calls=%fused_computation.65 | loop fusion | flops 45088768 | bytes 10485780 | tf_op jit(solution)/shard_map/neg | solution.py:113
  261.5 85.8 %fusion.155 = (f32[]{:T(128)}, f32[]{:T(128)}) fusion(s32[]{:T(128)S(6)} %mul.5966, f32[1,2,262144]{2,1,0:T(2,128)S(1)} %multiply_add_fusion.3, f32[]{:T(128)} %bitcast.60, f32[]{:T(128)} %bitcast.59, f32[1,2,262144]{2,1,0:T(2,128)S(1)} %copy-done, f32[]{:T(128)} %bitcast.58, f32[]{:T(128)} %bitcast.57, f32[]{:T(128)} %bitcast.56, f32[]{:T(128)} %bitcast.55, ...), kind=kLoop, calls=%fused_computation.310 | loop fusion | flops 66584576 | bytes 4194420 | tf_op jit(solution)/shard_map/reduce_sum | solution.py:102
  347.3 4.7 reshape.2348
  354.1 4.8 all-to-all-start.1
  360.2 5.8 convolution_bitcast_fusion.2
  365.9 4.7 reshape.2353
  370.6 7.7 fusion.19
  378.3 7.6 fusion.55
  386.0 4.2 reshape.2349
  390.2 4.3 reshape.2351
  397.0 9.5 %multiply_add_fusion.2 = f32[1,2,262144]{2,1,0:T(2,128)S(1)} fusion(f32[1,2,262144]{2,1,0:T(2,128)} %collective-permute-done.7, f32[1,2,262144]{2,1,0:T(2,128)} %collective-permute-done.6, f32[1,2,262144]{2,1,0:T(2,128)} %collective-permute-done.5, f32[1,2,262144]{2,1,0:T(2,128)} %collective-permute-done.4, f32[1,2,262144]{2,1,0:T(2,128)} %reshape.2353, ...), kind=kLoop, calls=%fused_computation.34 | loop fusion | flops 5242880 | bytes 16777232 | tf_op jit(solution)/shard_map/add | solution.py:99
  406.5 51.7 %add_multiply_fusion.5 = (f32[1,1,262144]{2,1,0:T(1,128)S(1)}, f32[1,1,262144]{2,1,0:T(1,128)S(1)}, f32[1,1,262144]{2,1,0:T(1,128)}, f32[1,1,262144]{2,1,0:T(1,128)}) fusion(f32[1,1,262144]{2,1,0:T(1,128)S(1)} %copy-done.2, f32[1,1,262144]{2,1,0:T(1,128)S(1)} %get-tuple-element.13, f32[1,1,262144]{2,1,0:T(1,128)S(1)} %copy-done.4, f32[]{:T(128)} %bitcast.81, ...), kind=kLoop, calls=%fused_computation.96 | loop fusion | flops 47972352 | bytes 9437204 | tf_op jit(solution)/shard_map/mul | solution.py:115
  462.4 4.8 reshape.2354
  473.5 26.5 %fusion.41 = (f32[]{:T(128)}, f32[]{:T(128)}, f32[262144]{0:T(1024)}, f32[262144]{0:T(1024)}, f32[262144]{0:T(1024)}) fusion(s32[]{:T(128)S(6)} %mul.5966, f32[]{:T(128)} %bitcast.81, f32[]{:T(128)} %bitcast.80, f32[262144]{0:T(1024)} %bitcast.350, f32[262144]{0:T(1024)} %bitcast.341, f32[262144]{0:T(1024)S(1)} %bitcast.340, f32[262144]{0:T(1024)} %bitcast.342, ...), kind=kLoop, calls=%fused_computation.186 | loop fusion | flops 73138176 | bytes 9437316 | tf_op jit(solution)/shard_map/reduce_sum | solution.py:102
  501.9 5.1 all-to-all-start.2
  508.3 5.8 convolution_bitcast_fusion.1
  514.0 4.7 reshape.2359
  518.8 7.7 fusion.18
  526.5 6.3 fusion.54
  535.5 4.4 reshape.2357
  539.9 20.0 %all-to-all-done.2 = f32[16,1,2]{2,1,0:T(1,128)S(1)} async-done(((f32[16,1,2]{2,1,0:T(1,128)}), f32[16,1,2]{2,1,0:T(1,128)S(1)}, u32[]{:S(2)}, u32[]{:S(2)}) %all-to-all-start.2) | async-done | bytes 160 | tf_op jit(solution)/shard_map/all_to_all | solution.py:16
  562.7 9.0 %multiply_add_fusion.1 = f32[1,2,262144]{2,1,0:T(2,128)S(1)} fusion(f32[1,2,262144]{2,1,0:T(2,128)} %collective-permute-done.11, f32[1,2,262144]{2,1,0:T(2,128)} %collective-permute-done.10, f32[1,2,262144]{2,1,0:T(2,128)} %collective-permute-done.9, f32[1,2,262144]{2,1,0:T(2,128)} %collective-permute-done.8, f32[1,2,262144]{2,1,0:T(2,128)S(1)} %copy-done.12, ...), kind=kLoop, calls=%fused_computation.33 | loop fusion | flops 5242880 | bytes 16777232 | tf_op jit(solution)/shard_map/add | solution.py:99
  571.7 51.7 %add_multiply_fusion.3 = (f32[1,1,262144]{2,1,0:T(1,128)S(1)}, f32[1,1,262144]{2,1,0:T(1,128)S(1)}, f32[1,1,262144]{2,1,0:T(1,128)}, f32[1,1,262144]{2,1,0:T(1,128)}) fusion(f32[1,1,262144]{2,1,0:T(1,128)S(1)} %copy-done.11, f32[1,1,262144]{2,1,0:T(1,128)S(1)} %copy-done.8, f32[1,1,262144]{2,1,0:T(1,128)S(1)} %copy-done.5, f32[]{:T(128)} %bitcast.97, ...), kind=kLoop, calls=%fused_computation.92 | loop fusion | flops 47972352 | bytes 9437204 | tf_op jit(solution)/shard_map/mul | solution.py:115
  631.9 4.7 reshape.2360
  636.6 8.5 %fusion.154 = (f32[]{:T(128)}, f32[]{:T(128)}) fusion(s32[]{:T(128)S(6)} %mul.5966, f32[262144]{0:T(1024)} %get-tuple-element.11, f32[262144]{0:T(1024)} %get-tuple-element.10, f32[262144]{0:T(1024)} %bitcast.352, f32[262144]{0:T(1024)} %get-tuple-element.12, f32[]{:T(128)} %bitcast.97, f32[]{:T(128)} %bitcast.96, f32[262144]{0:T(1024)} %bitcast.351, ...), kind=kLoop, calls=%fused_computation.309 | loop fusion | flops 49020928 | bytes 5242908 | tf_op jit(solution)/shard_map/reduce_sum | solution.py:102
  647.0 6.5 all-to-all-start.3
  654.7 5.7 convolution_bitcast_fusion
  660.4 7.7 fusion.17
  668.1 7.6 fusion.53
  675.7 4.7 reshape.2365
  680.4 4.2 reshape.2363
  684.6 32.0 %all-to-all-done.3 = f32[16,1,2]{2,1,0:T(1,128)S(1)} async-done(((f32[16,1,2]{2,1,0:T(1,128)}), f32[16,1,2]{2,1,0:T(1,128)S(1)}, u32[]{:S(2)}, u32[]{:S(2)}) %all-to-all-start.3) | async-done | bytes 160 | tf_op jit(solution)/shard_map/all_to_all | solution.py:16
  718.6 4.2 reshape.2361
  722.8 19.5 %psum.7 = f32[4,2]{0,1:T(2,128)} all-reduce(f32[4,2]{0,1:T(2,128)S(1)} %maximum_maximum_fusion), channel_id=1, replica_groups=mesh['gx'=16,'gy'=8] {'gy'}, use_global_device_ids=true, to_apply=%region_12.0 | all-reduce | flops 8 | bytes 64 | tf_op jit(solution)/shard_map/psum | solution.py:131
  743.1 9.2 %multiply_add_fusion = f32[1,2,262144]{2,1,0:T(2,128)S(1)} fusion(f32[1,2,262144]{2,1,0:T(2,128)} %collective-permute-done.15, f32[1,2,262144]{2,1,0:T(2,128)} %collective-permute-done.14, f32[1,2,262144]{2,1,0:T(2,128)} %collective-permute-done.13, f32[1,2,262144]{2,1,0:T(2,128)} %collective-permute-done.12, f32[1,2,262144]{2,1,0:T(2,128)} %reshape.2365, ...), kind=kLoop, calls=%fused_computation.32 | loop fusion | flops 5242880 | bytes 16777232 | tf_op jit(solution)/shard_map/add | solution.py:99
  752.3 50.8 %add_multiply_fusion.1 = (f32[1,1,262144]{2,1,0:T(1,128)S(1)}, f32[1,1,262144]{2,1,0:T(1,128)S(1)}) fusion(f32[1,1,262144]{2,1,0:T(1,128)S(1)} %get-tuple-element.18, f32[1,1,262144]{2,1,0:T(1,128)S(1)} %get-tuple-element.17, f32[1,1,262144]{2,1,0:T(1,128)S(1)} %copy-done.5, f32[1,2,262144]{2,1,0:T(2,128)S(1)} %multiply_add_fusion, f32[]{:T(128)} %bitcast.112, ...), kind=kLoop, calls=%fused_computation.90 | loop fusion | flops 47972352 | bytes 7340052 | tf_op jit(solution)/shard_map/mul | solution.py:115
  (110 shorter events, 57.0 us)
Async XLA Ops:
  0.6 60.7 %copy-start = (f32[1,2,262144]{2,1,0:T(2,128)S(1)}, f32[1,2,262144]{2,1,0:T(2,128)}, u32[]{:S(2)}) copy-start(f32[1,2,262144]{2,1,0:T(2,128)} %param.4) | copy-start | bytes 6291460
  0.6 113.8 %collective-permute-start.1 = (f32[1,2,262144]{2,1,0:T(2,128)}, f32[1,2,262144]{2,1,0:T(2,128)}, u32[]{:S(2)}, u32[]{:S(2)}) collective-permute-start(f32[1,2,262144]{2,1,0:T(2,128)} %param.4), channel_id=1, source_target_pairs={{0,16},{8,24},{16,0},{24,8},{32,48},{40,56},{48,32},{56,40},{64,80... | collective-permute-start | bytes 6291464 | tf_op jit(solution)/shard_map/ppermute | solution.py:11
  5.1 109.3 %collective-permute-start = (f32[1,2,262144]{2,1,0:T(2,128)}, f32[1,2,262144]{2,1,0:T(2,128)}, u32[]{:S(2)}, u32[]{:S(2)}) collective-permute-start(f32[1,2,262144]{2,1,0:T(2,128)} %param.4), channel_id=1, source_target_pairs={{0,8},{8,0},{16,24},{24,16},{32,40},{40,32},{48,56},{56,48},{64,72... | collective-permute-start | bytes 6291464 | tf_op jit(solution)/shard_map/ppermute | solution.py:11
  5.9 108.6 %collective-permute-start.3 = (f32[1,2,262144]{2,1,0:T(2,128)}, f32[1,2,262144]{2,1,0:T(2,128)}, u32[]{:S(2)}, u32[]{:S(2)}) collective-permute-start(f32[1,2,262144]{2,1,0:T(2,128)} %param.4), channel_id=1, source_target_pairs={{0,64},{8,72},{16,80},{24,88},{32,96},{40,104},{48,112},{56,120},{... | collective-permute-start | bytes 6291464 | tf_op jit(solution)/shard_map/ppermute | solution.py:11
  8.8 105.7 %collective-permute-start.2 = (f32[1,2,262144]{2,1,0:T(2,128)}, f32[1,2,262144]{2,1,0:T(2,128)}, u32[]{:S(2)}, u32[]{:S(2)}) collective-permute-start(f32[1,2,262144]{2,1,0:T(2,128)} %param.4), channel_id=1, source_target_pairs={{0,32},{8,40},{16,48},{24,56},{32,0},{40,8},{48,16},{56,24},{64,96... | collective-permute-start | bytes 6291464 | tf_op jit(solution)/shard_map/ppermute | solution.py:11
  57.6 54.1 %all-to-all-start = ((f32[16,1,2]{2,1,0:T(1,128)}), f32[16,1,2]{2,1,0:T(1,128)S(1)}, u32[]{:S(2)}, u32[]{:S(2)}) async-start(f32[16,1,2]{2,1,0:T(1,128)} %broadcast_in_dim.8), calls=%async_computation | async-start | bytes 16384 | tf_op jit(solution)/shard_map/all_to_all | solution.py:16
  61.3 3.2 copy-start.20
  61.4 7.7 copy-start.18
  88.8 4.9 copy-start.19
  203.0 49.4 %copy-start.3 = (f32[1,1,262144]{2,1,0:T(1,128)}, f32[1,1,262144]{2,1,0:T(1,128)S(1)}, u32[]{:S(2)}) copy-start(f32[1,1,262144]{2,1,0:T(1,128)S(1)} %get-tuple-element.14) | copy-start | bytes 3145732
  252.5 2.9 copy-start.1
  255.4 141.5 %collective-permute-start.7 = (f32[1,2,262144]{2,1,0:T(2,128)}, f32[1,2,262144]{2,1,0:T(2,128)}, u32[]{:S(2)}, u32[]{:S(2)}) collective-permute-start(f32[1,2,262144]{2,1,0:T(2,128)} %pad_maximum_fusion), channel_id=1, source_target_pairs={{0,64},{8,72},{16,80},{24,88},{32,96},{40,104},{48,112},{56,120},{... | collective-permute-start | bytes 6291464 | tf_op jit(solution)/shard_map/ppermute | solution.py:11
  258.2 138.7 %collective-permute-start.6 = (f32[1,2,262144]{2,1,0:T(2,128)}, f32[1,2,262144]{2,1,0:T(2,128)}, u32[]{:S(2)}, u32[]{:S(2)}) collective-permute-start(f32[1,2,262144]{2,1,0:T(2,128)} %pad_maximum_fusion), channel_id=1, source_target_pairs={{0,32},{8,40},{16,48},{24,56},{32,0},{40,8},{48,16},{56,24},{64,96... | collective-permute-start | bytes 6291464 | tf_op jit(solution)/shard_map/ppermute | solution.py:11
  258.5 138.4 %collective-permute-start.5 = (f32[1,2,262144]{2,1,0:T(2,128)}, f32[1,2,262144]{2,1,0:T(2,128)}, u32[]{:S(2)}, u32[]{:S(2)}) collective-permute-start(f32[1,2,262144]{2,1,0:T(2,128)} %pad_maximum_fusion), channel_id=1, source_target_pairs={{0,16},{8,24},{16,0},{24,8},{32,48},{40,56},{48,32},{56,40},{64,80... | collective-permute-start | bytes 6291464 | tf_op jit(solution)/shard_map/ppermute | solution.py:11
  261.2 135.7 %collective-permute-start.4 = (f32[1,2,262144]{2,1,0:T(2,128)}, f32[1,2,262144]{2,1,0:T(2,128)}, u32[]{:S(2)}, u32[]{:S(2)}) collective-permute-start(f32[1,2,262144]{2,1,0:T(2,128)} %pad_maximum_fusion), channel_id=1, source_target_pairs={{0,8},{8,0},{16,24},{24,16},{32,40},{40,32},{48,56},{56,48},{64,72... | collective-permute-start | bytes 6291464 | tf_op jit(solution)/shard_map/ppermute | solution.py:11
  352.0 7.5 copy-start.2
  354.1 40.4 %all-to-all-start.1 = ((f32[16,1,2]{2,1,0:T(1,128)}), f32[16,1,2]{2,1,0:T(1,128)S(1)}, u32[]{:S(2)}, u32[]{:S(2)}) async-start(f32[16,1,2]{2,1,0:T(1,128)} %broadcast_in_dim.9), calls=%async_computation.1 | async-start | bytes 16384 | tf_op jit(solution)/shard_map/all_to_all | solution.py:16
  370.6 7.7 copy-start.15
  396.9 9.6 %copy-start.4 = (f32[1,1,262144]{2,1,0:T(1,128)S(1)}, f32[1,1,262144]{2,1,0:T(1,128)}, u32[]{:S(2)}) copy-start(f32[1,1,262144]{2,1,0:T(1,128)} %copy-done.3) | copy-start | bytes 3145732
  458.1 1.1 copy-start.6
  458.1 1.4 copy-start.9
  462.4 11.1 %copy-start.16 = (f32[1,1,262144]{2,1,0:T(1,128)S(1)}, f32[1,1,262144]{2,1,0:T(1,128)}, u32[]{:S(2)}) copy-start(f32[1,1,262144]{2,1,0:T(1,128)} %get-tuple-element.24) | copy-start | bytes 3145732
  462.4 11.1 %copy-start.17 = (f32[1,1,262144]{2,1,0:T(1,128)S(1)}, f32[1,1,262144]{2,1,0:T(1,128)}, u32[]{:S(2)}) copy-start(f32[1,1,262144]{2,1,0:T(1,128)} %get-tuple-element.26) | copy-start | bytes 3145732
  467.2 95.4 %collective-permute-start.11 = (f32[1,2,262144]{2,1,0:T(2,128)}, f32[1,2,262144]{2,1,0:T(2,128)}, u32[]{:S(2)}, u32[]{:S(2)}) collective-permute-start(f32[1,2,262144]{2,1,0:T(2,128)} %pad_maximum_fusion.1), channel_id=1, source_target_pairs={{0,64},{8,72},{16,80},{24,88},{32,96},{40,104},{48,112},{56,120},{... | collective-permute-start | bytes 6291464 | tf_op jit(solution)/shard_map/ppermute | solution.py:11
  470.2 92.4 %collective-permute-start.10 = (f32[1,2,262144]{2,1,0:T(2,128)}, f32[1,2,262144]{2,1,0:T(2,128)}, u32[]{:S(2)}, u32[]{:S(2)}) collective-permute-start(f32[1,2,262144]{2,1,0:T(2,128)} %pad_maximum_fusion.1), channel_id=1, source_target_pairs={{0,32},{8,40},{16,48},{24,56},{32,0},{40,8},{48,16},{56,24},{64,96... | collective-permute-start | bytes 6291464 | tf_op jit(solution)/shard_map/ppermute | solution.py:11
  470.5 92.1 %collective-permute-start.9 = (f32[1,2,262144]{2,1,0:T(2,128)}, f32[1,2,262144]{2,1,0:T(2,128)}, u32[]{:S(2)}, u32[]{:S(2)}) collective-permute-start(f32[1,2,262144]{2,1,0:T(2,128)} %pad_maximum_fusion.1), channel_id=1, source_target_pairs={{0,16},{8,24},{16,0},{24,8},{32,48},{40,56},{48,32},{56,40},{64,80... | collective-permute-start | bytes 6291464 | tf_op jit(solution)/shard_map/ppermute | solution.py:11
  473.2 89.5 %collective-permute-start.8 = (f32[1,2,262144]{2,1,0:T(2,128)}, f32[1,2,262144]{2,1,0:T(2,128)}, u32[]{:S(2)}, u32[]{:S(2)}) collective-permute-start(f32[1,2,262144]{2,1,0:T(2,128)} %pad_maximum_fusion.1), channel_id=1, source_target_pairs={{0,8},{8,0},{16,24},{24,16},{32,40},{40,32},{48,56},{56,48},{64,72... | collective-permute-start | bytes 6291464 | tf_op jit(solution)/shard_map/ppermute | solution.py:11
  473.5 33.6 %copy-start.10 = (f32[1,1,262144]{2,1,0:T(1,128)S(1)}, f32[1,1,262144]{2,1,0:T(1,128)}, u32[]{:S(2)}) copy-start(f32[1,1,262144]{2,1,0:T(1,128)} %copy-done.9) | copy-start | bytes 3145732
  500.0 7.7 copy-start.7
  501.9 58.0 %all-to-all-start.2 = ((f32[16,1,2]{2,1,0:T(1,128)}), f32[16,1,2]{2,1,0:T(1,128)S(1)}, u32[]{:S(2)}, u32[]{:S(2)}) async-start(f32[16,1,2]{2,1,0:T(1,128)} %broadcast_in_dim.10), calls=%async_computation.2 | async-start | bytes 16384 | tf_op jit(solution)/shard_map/all_to_all | solution.py:16
  518.8 7.7 copy-start.13
  535.5 27.2 %copy-start.12 = (f32[1,2,262144]{2,1,0:T(2,128)S(1)}, f32[1,2,262144]{2,1,0:T(2,128)}, u32[]{:S(2)}) copy-start(f32[1,2,262144]{2,1,0:T(2,128)} %reshape.2359) | copy-start | bytes 6291460
  562.6 9.1 %copy-start.5 = (f32[1,1,262144]{2,1,0:T(1,128)S(1)}, f32[1,1,262144]{2,1,0:T(1,128)}, u32[]{:S(2)}) copy-start(f32[1,1,262144]{2,1,0:T(1,128)} %copy-done.3) | copy-start | bytes 3145732
  562.6 9.1 %copy-start.8 = (f32[1,1,262144]{2,1,0:T(1,128)S(1)}, f32[1,1,262144]{2,1,0:T(1,128)}, u32[]{:S(2)}) copy-start(f32[1,1,262144]{2,1,0:T(1,128)} %copy-done.6) | copy-start | bytes 3145732
  562.6 9.1 %copy-start.11 = (f32[1,1,262144]{2,1,0:T(1,128)S(1)}, f32[1,1,262144]{2,1,0:T(1,128)}, u32[]{:S(2)}) copy-start(f32[1,1,262144]{2,1,0:T(1,128)} %copy-done.9) | copy-start | bytes 3145732
  626.2 116.8 %collective-permute-start.15 = (f32[1,2,262144]{2,1,0:T(2,128)}, f32[1,2,262144]{2,1,0:T(2,128)}, u32[]{:S(2)}, u32[]{:S(2)}) collective-permute-start(f32[1,2,262144]{2,1,0:T(2,128)} %pad_maximum_fusion.2), channel_id=1, source_target_pairs={{0,64},{8,72},{16,80},{24,88},{32,96},{40,104},{48,112},{56,120},{... | collective-permute-start | bytes 6291464 | tf_op jit(solution)/shard_map/ppermute | solution.py:11
  628.5 114.6 %collective-permute-start.14 = (f32[1,2,262144]{2,1,0:T(2,128)}, f32[1,2,262144]{2,1,0:T(2,128)}, u32[]{:S(2)}, u32[]{:S(2)}) collective-permute-start(f32[1,2,262144]{2,1,0:T(2,128)} %pad_maximum_fusion.2), channel_id=1, source_target_pairs={{0,32},{8,40},{16,48},{24,56},{32,0},{40,8},{48,16},{56,24},{64,96... | collective-permute-start | bytes 6291464 | tf_op jit(solution)/shard_map/ppermute | solution.py:11
  628.7 114.4 %collective-permute-start.13 = (f32[1,2,262144]{2,1,0:T(2,128)}, f32[1,2,262144]{2,1,0:T(2,128)}, u32[]{:S(2)}, u32[]{:S(2)}) collective-permute-start(f32[1,2,262144]{2,1,0:T(2,128)} %pad_maximum_fusion.2), channel_id=1, source_target_pairs={{0,16},{8,24},{16,0},{24,8},{32,48},{40,56},{48,32},{56,40},{64,80... | collective-permute-start | bytes 6291464 | tf_op jit(solution)/shard_map/ppermute | solution.py:11
  630.3 112.8 %collective-permute-start.12 = (f32[1,2,262144]{2,1,0:T(2,128)}, f32[1,2,262144]{2,1,0:T(2,128)}, u32[]{:S(2)}, u32[]{:S(2)}) collective-permute-start(f32[1,2,262144]{2,1,0:T(2,128)} %pad_maximum_fusion.2), channel_id=1, source_target_pairs={{0,8},{8,0},{16,24},{24,16},{32,40},{40,32},{48,56},{56,48},{64,72... | collective-permute-start | bytes 6291464 | tf_op jit(solution)/shard_map/ppermute | solution.py:11
  647.0 69.6 %all-to-all-start.3 = ((f32[16,1,2]{2,1,0:T(1,128)}), f32[16,1,2]{2,1,0:T(1,128)S(1)}, u32[]{:S(2)}, u32[]{:S(2)}) async-start(f32[16,1,2]{2,1,0:T(1,128)} %broadcast_in_dim.11), calls=%async_computation.3 | async-start | bytes 16384 | tf_op jit(solution)/shard_map/all_to_all | solution.py:16
  660.4 7.7 copy-start.14
where the time goes:
time: 812 us; the launch traced here: 806 us
  other arithmetic  504 us (62%)
  matrix products  85.5 us (11%)
  local copies, waits for them, and re-layouts  85 us (10%)
  waiting for transfers between devices  52.1 us (6%)
  starting transfers between devices  45.3 us (6%)
  blocking collectives  19.5 us (2%)
  between operations  14.5 us (2%)
    mul x4, other arithmetic, shards(): factor * (keep * real_part + time_step * coherent_real + kick * (real_par...  233 us
    reduce_sum x4, other arithmetic, shards(): jnp.sum(weight, axis=1)  167 us
    dot_general x8, matrix products, block_flip(): jnp.einsum('pcakb,kj->pcajb', viewed, table, precision=lax.Precision.HIGH...  54.6 us
    all_to_all x4, waiting for transfers between devices, sent_to_all(): lax.all_to_all(jnp.broadcast_to(array[None], (length, *array.shape)), axi...  52 us
    neg x1, other arithmetic, shards(): coherent_real = -result[:, 1] - energy[None, :] * imag_part  49.4 us
    add x4, other arithmetic, shards(): result = result + fields[low_bits + b] * from_partner(amplitudes, 'gx', b)  36.9 us
    reshape x8, local copies, waits for them, and re-layouts, block_flip(): return result.reshape(shape)  35.9 us
    dot_general x4, matrix products, block_flip(): jnp.dot(amplitudes.reshape(-1, 1 << width), table, precision=lax.Precisio...  30.9 us
  transfers between devices with their start and end apart: 20, of which 2 were waited for; matrix products, arithmetic and copies ran while one was open for 42% of the time, Pallas kernels for 0%

commit v1 on v0

v1 whole, which is shorter than its diff:
```python
import functools

import jax
import jax.numpy as jnp
from jax import lax
from jax.experimental import pallas as pl
from jax.experimental.pallas import tpu as pltpu
from jax.sharding import PartitionSpec as P

MESH = pl.DeviceIdType.MESH
KAPPA = 4.0
DT = 0.05
NQ = 22
DIM = 4194304
SUBS = 4
F32 = jnp.float32


def kernel(
    fields, couplings, noise, x_ref, o_ref, rec_ref,
    bp, v1b, v1a, v2b, v2a, psi1, tee, flips, why, psi2,
    table, occ_base, en_base, scal, red_src, red_dst, rec_src, rec_dst, energies, pops,
    send_sem, recv_sem, red_send, red_recv, rec_send, rec_recv,
):
    me = lax.axis_index("gx")
    gy = lax.axis_index("gy")
    n_gx, n_gy = 16, 8

    barrier = pltpu.get_barrier_semaphore()

    def greet(k, _):
        pl.semaphore_signal(barrier, inc=1, device_id=(me ^ k, gy), device_id_type=MESH)
        return 0

    def greet_y(k, _):
        pl.semaphore_signal(barrier, inc=1, device_id=(me, gy ^ k), device_id_type=MESH)
        return 0

    lax.fori_loop(1, n_gx, greet, 0)
    lax.fori_loop(1, n_gy, greet_y, 0)

    shape3 = (8, 8, 128)
    sub = lax.broadcasted_iota(jnp.int32, (8, 128), 0)
    lane = lax.broadcasted_iota(jnp.int32, (8, 128), 1)
    even = (sub & 1) == 0
    sign = jnp.where(even, -1.0, 1.0).astype(F32)
    bit1 = (sub & 2) == 0
    even3 = jnp.broadcast_to(even[None], shape3)
    bit1_3 = jnp.broadcast_to(bit1[None], shape3)
    z0 = 1.0 - 2.0 * (lane & 1).astype(F32)

    def times_i(y):
        return sign[None] * jnp.where(even3, pltpu.roll(y, 7, 1), pltpu.roll(y, 1, 1))

    rows = lax.broadcasted_iota(jnp.int32, (128, 128), 0)
    cols = lax.broadcasted_iota(jnp.int32, (128, 128), 1)
    diff = rows ^ cols
    flip_table = jnp.zeros((128, 128), F32)
    for q in range(7):
        flip_table = jnp.where(diff == 1 << q, fields[q], flip_table)
    table[...] = flip_table
    for u in range(8):
        low = lane | ((sub >> 1) << 7) | (u << 9)
        pair = low ^ (low >> 1)
        pop = jnp.zeros((8, 128), jnp.int32)
        energy = jnp.zeros((8, 128), F32)
        for q in range(12):
            pop = pop + ((low >> q) & 1)
        for q in range(11):
            energy = energy + couplings[q] * (1.0 - 2.0 * ((pair >> q) & 1).astype(F32))
        occ_base[u] = pop.astype(F32) * (1.0 / NQ)
        en_base[u] = energy

    def fill(i, _):
        j, s = i >> 2, i & 3
        for which in range(2):
            k, d = (j, me) if which == 0 else (me, j)
            full = s | (k << 2) | (d << 6)
            pair = full ^ (full >> 1)
            total = F32(0.0)
            count = jnp.int32(0)
            for q in range(9):
                total = total + couplings[12 + q] * (1 - 2 * ((pair >> q) & 1)).astype(F32)
            for q in range(10):
                count = count + ((full >> q) & 1)
            energies[which * 64 + i] = total
            pops[which * 64 + i] = count.astype(F32) * (1.0 / NQ)
        return 0

    lax.fori_loop(0, 64, fill, 0)

    pl.semaphore_wait(barrier, n_gx - 1 + n_gy - 1)

    def send_group(src, dst, move, s):
        def one(k, _):
            other = me ^ k
            pltpu.make_async_remote_copy(
                src_ref=src.at[other, s], dst_ref=dst.at[me, s],
                send_sem=send_sem.at[move, s], recv_sem=recv_sem.at[move, s],
                device_id=(other, gy), device_id_type=MESH,
            ).start()
            return 0

        lax.fori_loop(1, n_gx, one, 0)

    def wait_bytes(ref, sem):
        pltpu.make_async_copy(ref, ref, sem).wait()

    def wait_group(dst, move, s):
        wait_bytes(dst.at[pl.ds(0, 15), s], recv_sem.at[move, s])

    def own(src, dst):
        def one(s, _):
            dst[me, s] = src[me, s]
            return 0

        lax.fori_loop(0, SUBS, one, 0)

    def reduce_send(step, norm8, mag8):
        both = jnp.concatenate(
            [jnp.sum(norm8, axis=0, keepdims=True), jnp.sum(mag8, axis=0, keepdims=True)], axis=0
        )
        red_src[step] = both
        red_dst[step, me] = both

        def one(k, _):
            pltpu.make_async_remote_copy(
                src_ref=red_src.at[step], dst_ref=red_dst.at[step, me],
                send_sem=red_send.at[step], recv_sem=red_recv.at[step],
                device_id=(me ^ k, gy), device_id_type=MESH,
            ).start()
            return 0

        lax.fori_loop(1, n_gx, one, 0)

    def reduce_wait(step):
        wait_bytes(red_dst.at[step, pl.ds(0, 15)], red_recv.at[step])
        total = jnp.sum(jnp.sum(red_dst[step], axis=0), axis=1, keepdims=True)
        norm, mag = total[0:1], total[1:2]
        scal[step, 0] = jnp.broadcast_to(mag / norm, (8, 128))
        scal[step, 1] = jnp.broadcast_to(jnp.sqrt(float(DIM) / norm), (8, 128))

    half_root = 0.15811388300841897

    def moved(step, which, index, psi, flip):
        mag, phi = scal[step, 0], scal[step, 1]
        x1 = noise[2 * step] * half_root
        x2 = noise[2 * step + 1] * half_root
        s = index & 3
        other = index >> 2
        d = me if which == 0 else other
        z12 = (1 - 2 * (s & 1)).astype(F32)
        z21 = (1 - 2 * ((d >> 3) & 1)).astype(F32)
        place = which * 64 + index
        edge = (couplings[21] * z21) * z0 + energies[place]
        off = pops[place] - mag
        turn = couplings[11] * z12
        parts = []
        for u in range(8):
            z11 = -1.0 if u & 4 else 1.0
            shift = occ_base[u] + off
            grow = phi * (1.0 + shift * (2.0 * x1 - (DT * KAPPA * 0.5) * shift))
            energy = en_base[u] + (edge + turn * z11)
            spin = phi * ((2.0 * x2) * shift + DT * energy)
            parts.append((grow, spin))
        grow = jnp.stack([p[0] for p in parts])
        spin = jnp.stack([p[1] for p in parts])
        return grow * psi + times_i(spin * psi + (DT * phi)[None] * flip)

    def weigh(index, psi, carry):
        norm8, mag8 = carry
        weight = psi * psi
        total = jnp.sum(weight, axis=0)
        part = jnp.sum(weight * occ_base[...], axis=0)
        return norm8 + total, mag8 + part + pops[index] * total

    zero8 = jnp.zeros((8, 128), F32)

    def local_flips(src, dst):
        def one(k, _):
            block = src[k]
            lanes = jnp.dot(
                block.reshape(256, 128), table[...],
                precision=lax.Precision.HIGHEST, preferred_element_type=F32,
            ).reshape(4, 8, 8, 128)
            for s in range(SUBS):
                here = block[s]
                total = lanes[s]
                total = total + fields[7] * jnp.where(
                    bit1_3, pltpu.roll(here, 6, 1), pltpu.roll(here, 2, 1)
                )
                total = total + fields[8] * pltpu.roll(here, 4, 1)
                for b in range(3):
                    total = total + fields[9 + b] * jnp.stack([here[u ^ (1 << b)] for u in range(8)])
                for b in range(2):
                    total = total + fields[12 + b] * block[s ^ (1 << b)]
                for b in range(4):
                    total = total + fields[14 + b] * src[k ^ (1 << b), s]
                dst[k, s] = total
            return 0

        lax.fori_loop(0, 16, one, 0)

    def high_flips(src, dst, s):
        def one(d, _):
            total = fields[18] * src[d ^ 1, s]
            for b in range(1, 4):
                total = total + fields[18 + b] * src[d ^ (1 << b), s]
            dst[d, s] = total
            return 0

        lax.fori_loop(0, 16, one, 0)

    def round_of(r, start, finish):
        base = 3 * r
        first, second = 2 * r, 2 * r + 1
        held, out1, in1, out2, in2 = bp.at[r], v1b.at[r], v1a.at[r], v2b.at[r], v2a.at[r]
        own(start, held)
        local_flips(start, flips)
        for s in range(SUBS):
            wait_group(held, base, s)
            high_flips(held, out1, s)
            send_group(out1, in1, base + 1, s)
        own(out1, in1)
        reduce_wait(first)
        for s in range(SUBS):

            def one(d, _):
                why[d, s] = moved(first, 1, d * 4 + s, held[d, s], out1[d, s])
                return 0

            lax.fori_loop(0, 16, one, 0)
            high_flips(why, out2, s)
            if s < 2:
                send_group(out2, in2, base + 2, s)
        own(out2, in2)
        carry = (zero8, zero8)
        for s in range(SUBS):
            wait_group(in1, base + 1, s)

            def one(k, carry):
                back = in1[k, s]
                new = moved(first, 0, k * 4 + s, start[k, s], flips[k, s] + back)
                psi1[k, s] = new
                tee[k, s] = new + times_i((DT * scal[first, 1])[None] * back)
                return weigh(k * 4 + s, new, carry)

            carry = lax.fori_loop(0, 16, one, carry)
        reduce_send(second, *carry)
        for s in range(2, SUBS):
            send_group(out2, in2, base + 2, s)
        local_flips(tee, flips)
        reduce_wait(second)
        if r == 1:
            send_record()
        carry = (zero8, zero8)
        for s in range(SUBS):
            wait_group(in2, base + 2, s)

            def one(k, carry):
                new = moved(second, 0, k * 4 + s, psi1[k, s], flips[k, s] + in2[k, s])
                finish[k, s] = new
                return weigh(k * 4 + s, new, carry) if r == 0 else carry

            carry = lax.fori_loop(0, 16, one, carry)
            if r == 0:
                send_group(finish, bp.at[1], 3, s)
        if r == 0:
            reduce_send(2, *carry)

    def send_record():
        total = zero8
        for step in range(4):
            kick = jnp.where(lane == 0, noise[2 * step], noise[2 * step + 1]) * half_root
            total = total + jnp.where(sub == step, (KAPPA ** 0.5 * DT) * scal[step, 0] + kick, 0.0)
        rec_src[...] = total
        rec_dst[gy] = total

        def one(k, _):
            pltpu.make_async_remote_copy(
                src_ref=rec_src, dst_ref=rec_dst.at[gy],
                send_sem=rec_send, recv_sem=rec_recv,
                device_id=(me, gy ^ k), device_id_type=MESH,
            ).start()
            return 0

        lax.fori_loop(1, n_gy, one, 0)

    for s in range(SUBS):
        send_group(x_ref, bp.at[0], 0, s)

    def first_weigh(i, carry):
        return weigh(i, x_ref[i >> 2, i & 3], carry)

    reduce_send(0, *lax.fori_loop(0, 64, first_weigh, (zero8, zero8)))
    round_of(0, x_ref, psi2)
    round_of(1, psi2, o_ref)

    wait_bytes(rec_dst.at[pl.ds(0, 7)], rec_recv)
    rec_ref[...] = jnp.sum(rec_dst[...], axis=0)[0:4, 0:2]

    for move in range(6):
        for s in range(SUBS):
            wait_bytes(bp.at[0, pl.ds(0, 15), s], send_sem.at[move, s])
    for step in range(4):
        wait_bytes(red_dst.at[step, pl.ds(0, 15)], red_send.at[step])
    wait_bytes(rec_dst.at[pl.ds(0, 7)], rec_send)


def shards(state, fields, couplings, noise):
    block = (16, SUBS, 8, 8, 128)
    x = state.reshape(2, 2048, 128).transpose(1, 0, 2).reshape(block)
    big = pltpu.VMEM(block, F32)
    pair = pltpu.VMEM((2, *block), F32)
    smem = pl.BlockSpec(memory_space=pltpu.SMEM)
    vmem = pl.BlockSpec(memory_space=pltpu.VMEM)
    final, record = pl.pallas_call(
        kernel,
        out_shape=(jax.ShapeDtypeStruct(block, F32), jax.ShapeDtypeStruct((4, 2), F32)),
        in_specs=[smem, smem, smem, vmem],
        out_specs=(vmem, vmem),
        scratch_shapes=[
            pair, pair, pair, pair, pair, big, big, big, big, big,
            pltpu.VMEM((128, 128), F32), pltpu.VMEM((8, 8, 128), F32), pltpu.VMEM((8, 8, 128), F32),
            pltpu.VMEM((4, 2, 8, 128), F32), pltpu.VMEM((4, 2, 128), F32), pltpu.VMEM((4, 16, 2, 128), F32),
            pltpu.VMEM((8, 128), F32), pltpu.VMEM((8, 8, 128), F32),
            pltpu.SMEM((128,), F32), pltpu.SMEM((128,), F32),
            pltpu.SemaphoreType.DMA((6, SUBS)), pltpu.SemaphoreType.DMA((6, SUBS)),
            pltpu.SemaphoreType.DMA((4,)), pltpu.SemaphoreType.DMA((4,)),
            pltpu.SemaphoreType.DMA, pltpu.SemaphoreType.DMA,
        ],
        compiler_params=pltpu.CompilerParams(
            collective_id=0, has_side_effects=True, vmem_limit_bytes=56 * 1024 * 1024
        ),
    )(fields, couplings, noise.reshape(8), x)
    final = final.reshape(2048, 2, 128).transpose(1, 0, 2).reshape(1, 2, 262144)
    return final, record


def solution(mesh):
    placed = (P("gy", None, "gx"), P(), P(), P("gy", None, None))
    return jax.shard_map(
        shards, mesh=mesh, in_specs=placed, out_specs=(P("gy", None, "gx"), P()), check_vma=False
    )
```

time: 812 us -> 159 us (0.20)
  other arithmetic: 504 us -> 0 us
  Pallas kernels: 0 us -> 153 us
  matrix products: 85.5 us -> 0 us
  local copies, waits for them, and re-layouts: 85 us -> 5.28 us
  waiting for transfers between devices: 52.1 us -> 0 us
  starting transfers between devices: 45.3 us -> 0 us
  blocking collectives: 19.5 us -> 0 us
  between operations: 14.5 us -> 0.64 us
    mul x4 -> x0, other arithmetic: 233 us -> none  [shards(): factor * (keep * real_part + time_step * coherent_real + kick * (real_par...]
    reduce_sum x8 -> x0, other arithmetic: 167 us -> none  [the longest x4 167 us: shards(): jnp.sum(weight, axis=1)]
    pallas_call x0 -> x1, Pallas kernels: none -> 153 us  [shards(): pl.pallas_call(kernel, out_shape=(jax.ShapeDtypeStruct(block, F32), jax.S...]
    dot_general x12 -> x0, matrix products: 85.5 us -> none  [the longest x8 54.6 us: block_flip(): jnp.einsum('pcakb,kj->pcajb', viewed, table, precision=lax.Precision.HIGH...]
    reshape x16 -> x1, local copies, waits for them, and re-layouts: 68.7 us -> 0.6 us  [shards(): noise.reshape(8)]
    all_to_all x4 -> x0, waiting for transfers between devices: 52 us -> none  [sent_to_all(): lax.all_to_all(jnp.broadcast_to(array[None], (length, *array.shape)), axi...]
    neg x1 -> x0, other arithmetic: 49.4 us -> none  [shards(): coherent_real = -result[:, 1] - energy[None, :] * imag_part]
    add x4 -> x0, other arithmetic: 36.9 us -> none  [shards(): result = result + fields[low_bits + b] * from_partner(amplitudes, 'gx', b)]
  transfers between devices with their start and end apart: 20 -> 0, of which waited for: 2 -> 0; matrix products, arithmetic and copies ran while one was open for 42% -> 0% of each run, Pallas kernels for 0% -> 0%
where the time goes in v1:
time: 159 us
  Pallas kernels  153 us (96%)
  local copies, waits for them, and re-layouts  5.28 us (3%)
    pallas_call x1, Pallas kernels, shards(): pl.pallas_call(kernel, out_shape=(jax.ShapeDtypeStruct(block, F32), jax.S...  153 us
    unnamed x3, local copies, waits for them, and re-layouts  4.68 us

profile of v1, /device:TPU:1, one launch (start us, length us, event | category | flops | bytes accessed | tf_op | source)
XLA Modules:
  0.0 158.7 jit_solution(13038121550489941969)
XLA Ops:
  0.6 0.8 copy.10
  1.4 0.6 reshape.19.noise
  2.0 152.8 %shard_map.59 = (f32[16,4,8,8,128]{4,3,2,1,0:T(8,128)}, f32[4,2]{1,0:T(4,128)}) custom-call(f32[22]{0:T(128)} %fields.1, f32[22]{0:T(128)} %couplings.1, f32[8]{0:T(128)} %reshape.19.noise, f32[16,4,8,8,128]{4,3,2,1,0:T(8,128)} %bitcast.10), custom_call_target="tpu_custom_call" | custom-call | tf_op jit(solution)/shard_map/pallas_call | solution.py:317
  154.8 1.3 copy.13
  156.1 2.6 %copy.15 = f32[1,2,262144]{2,1,0:T(2,128)} copy(f32[1,2,262144]{2,1,0:T(2,128)} %bitcast.11) | data formatting | bytes 4194304

commit v2 on v1

--- a/solution.py
+++ b/solution.py
@@ -13,14 +13,15 @@
 NQ = 22
 DIM = 4194304
 SUBS = 4
+WINDOW = 4
 F32 = jnp.float32
 
 
 def kernel(
-    fields, couplings, noise, x_ref, o_ref, rec_ref,
-    bp, v1b, v1a, v2b, v2a, psi1, tee, flips, why, psi2,
+    fields, couplings, noise, x_hbm, o_ref, rec_ref,
+    x_ref, bp, v1b, v1a, v2b, v2a, psi1, tee, flips, why, psi2,
     table, occ_base, en_base, scal, red_src, red_dst, rec_src, rec_dst, energies, pops,
-    send_sem, recv_sem, red_send, red_recv, rec_send, rec_recv,
+    send_sem, recv_sem, red_send, red_recv, rec_send, rec_recv, load_sem,
 ):
     me = lax.axis_index("gx")
     gy = lax.axis_index("gy")
@@ -36,6 +37,8 @@
         pl.semaphore_signal(barrier, inc=1, device_id=(me, gy ^ k), device_id_type=MESH)
         return 0
 
+    load = pltpu.make_async_copy(x_hbm, x_ref, load_sem)
+    load.start()
     lax.fori_loop(1, n_gx, greet, 0)
     lax.fori_loop(1, n_gy, greet_y, 0)
 
@@ -52,46 +55,19 @@
     def times_i(y):
         return sign[None] * jnp.where(even3, pltpu.roll(y, 7, 1), pltpu.roll(y, 1, 1))
 
-    rows = lax.broadcasted_iota(jnp.int32, (128, 128), 0)
-    cols = lax.broadcasted_iota(jnp.int32, (128, 128), 1)
-    diff = rows ^ cols
-    flip_table = jnp.zeros((128, 128), F32)
-    for q in range(7):
-        flip_table = jnp.where(diff == 1 << q, fields[q], flip_table)
-    table[...] = flip_table
-    for u in range(8):
-        low = lane | ((sub >> 1) << 7) | (u << 9)
-        pair = low ^ (low >> 1)
-        pop = jnp.zeros((8, 128), jnp.int32)
-        energy = jnp.zeros((8, 128), F32)
-        for q in range(12):
-            pop = pop + ((low >> q) & 1)
-        for q in range(11):
-            energy = energy + couplings[q] * (1.0 - 2.0 * ((pair >> q) & 1).astype(F32))
-        occ_base[u] = pop.astype(F32) * (1.0 / NQ)
-        en_base[u] = energy
-
-    def fill(i, _):
-        j, s = i >> 2, i & 3
-        for which in range(2):
-            k, d = (j, me) if which == 0 else (me, j)
-            full = s | (k << 2) | (d << 6)
-            pair = full ^ (full >> 1)
-            total = F32(0.0)
-            count = jnp.int32(0)
-            for q in range(9):
-                total = total + couplings[12 + q] * (1 - 2 * ((pair >> q) & 1)).astype(F32)
-            for q in range(10):
-                count = count + ((full >> q) & 1)
-            energies[which * 64 + i] = total
-            pops[which * 64 + i] = count.astype(F32) * (1.0 / NQ)
-        return 0
-
-    lax.fori_loop(0, 64, fill, 0)
-
+    load.wait()
     pl.semaphore_wait(barrier, n_gx - 1 + n_gy - 1)
 
+    issued = []
+
+    def wait_sent(move, s):
+        wait_bytes(bp.at[0, pl.ds(0, 15), s], send_sem.at[move, s])
+
     def send_group(src, dst, move, s):
+        if len(issued) >= WINDOW:
+            wait_sent(*issued[-WINDOW])
+        issued.append((move, s))
+
         def one(k, _):
             other = me ^ k
             pltpu.make_async_remote_copy(
@@ -144,8 +120,8 @@
 
     def moved(step, which, index, psi, flip):
         mag, phi = scal[step, 0], scal[step, 1]
-        x1 = noise[2 * step] * half_root
-        x2 = noise[2 * step + 1] * half_root
+        x1 = noise[0, step] * half_root
+        x2 = noise[1, step] * half_root
         s = index & 3
         other = index >> 2
         d = me if which == 0 else other
@@ -176,7 +152,7 @@
 
     zero8 = jnp.zeros((8, 128), F32)
 
-    def local_flips(src, dst):
+    def local_flips(src, dst, lo=0, hi=16):
         def one(k, _):
             block = src[k]
             lanes = jnp.dot(
@@ -199,7 +175,7 @@
                 dst[k, s] = total
             return 0
 
-        lax.fori_loop(0, 16, one, 0)
+        lax.fori_loop(lo, hi, one, 0)
 
     def high_flips(src, dst, s):
         def one(d, _):
@@ -216,7 +192,10 @@
         first, second = 2 * r, 2 * r + 1
         held, out1, in1, out2, in2 = bp.at[r], v1b.at[r], v1a.at[r], v2b.at[r], v2a.at[r]
         own(start, held)
-        local_flips(start, flips)
+        for s in range(2):
+            if r == 0:
+                send_group(start, held, 0, 2 + s)
+            local_flips(start, flips, 8 * s, 8 * s + 8)
         for s in range(SUBS):
             wait_group(held, base, s)
             high_flips(held, out1, s)
@@ -253,12 +232,20 @@
         reduce_wait(second)
         if r == 1:
             send_record()
+
+        def ready(i, _):
+            k, s = i >> 2, i & 3
+            psi1[k, s] = moved(second, 0, i, psi1[k, s], flips[k, s])
+            return 0
+
+        lax.fori_loop(0, 64, ready, 0)
+        turn = (DT * scal[second, 1])[None]
         carry = (zero8, zero8)
         for s in range(SUBS):
             wait_group(in2, base + 2, s)
 
             def one(k, carry):
-                new = moved(second, 0, k * 4 + s, psi1[k, s], flips[k, s] + in2[k, s])
+                new = psi1[k, s] + times_i(turn * in2[k, s])
                 finish[k, s] = new
                 return weigh(k * 4 + s, new, carry) if r == 0 else carry
 
@@ -271,8 +258,8 @@
     def send_record():
         total = zero8
         for step in range(4):
-            kick = jnp.where(lane == 0, noise[2 * step], noise[2 * step + 1]) * half_root
-            total = total + jnp.where(sub == step, (KAPPA ** 0.5 * DT) * scal[step, 0] + kick, 0.0)
+            kick = jnp.where(sub == 0, noise[0, step], noise[1, step]) * half_root
+            total = total + jnp.where(lane == step, (KAPPA ** 0.5 * DT) * scal[step, 0] + kick, 0.0)
         rec_src[...] = total
         rec_dst[gy] = total
 
@@ -286,8 +273,45 @@
 
         lax.fori_loop(1, n_gy, one, 0)
 
-    for s in range(SUBS):
+    for s in range(2):
         send_group(x_ref, bp.at[0], 0, s)
+
+    rows = lax.broadcasted_iota(jnp.int32, (128, 128), 0)
+    cols = lax.broadcasted_iota(jnp.int32, (128, 128), 1)
+    diff = rows ^ cols
+    flip_table = jnp.zeros((128, 128), F32)
+    for q in range(7):
+        flip_table = jnp.where(diff == 1 << q, fields[q], flip_table)
+    table[...] = flip_table
+    for u in range(8):
+        low = lane | ((sub >> 1) << 7) | (u << 9)
+        pair = low ^ (low >> 1)
+        pop = jnp.zeros((8, 128), jnp.int32)
+        energy = jnp.zeros((8, 128), F32)
+        for q in range(12):
+            pop = pop + ((low >> q) & 1)
+        for q in range(11):
+            energy = energy + couplings[q] * (1.0 - 2.0 * ((pair >> q) & 1).astype(F32))
+        occ_base[u] = pop.astype(F32) * (1.0 / NQ)
+        en_base[u] = energy
+
+    def fill(i, _):
+        j, s = i >> 2, i & 3
+        for which in range(2):
+            k, d = (j, me) if which == 0 else (me, j)
+            full = s | (k << 2) | (d << 6)
+            pair = full ^ (full >> 1)
+            total = F32(0.0)
+            count = jnp.int32(0)
+            for q in range(9):
+                total = total + couplings[12 + q] * (1 - 2 * ((pair >> q) & 1)).astype(F32)
+            for q in range(10):
+                count = count + ((full >> q) & 1)
+            energies[which * 64 + i] = total
+            pops[which * 64 + i] = count.astype(F32) * (1.0 / NQ)
+        return 0
+
+    lax.fori_loop(0, 64, fill, 0)
 
     def first_weigh(i, carry):
         return weigh(i, x_ref[i >> 2, i & 3], carry)
@@ -297,11 +321,10 @@
     round_of(1, psi2, o_ref)
 
     wait_bytes(rec_dst.at[pl.ds(0, 7)], rec_recv)
-    rec_ref[...] = jnp.sum(rec_dst[...], axis=0)[0:4, 0:2]
-
-    for move in range(6):
-        for s in range(SUBS):
-            wait_bytes(bp.at[0, pl.ds(0, 15), s], send_sem.at[move, s])
+    rec_ref[...] = jnp.sum(rec_dst[...], axis=0)[0:2, 0:4]
+
+    for pair in issued[-WINDOW:]:
+        wait_sent(*pair)
     for step in range(4):
         wait_bytes(red_dst.at[step, pl.ds(0, 15)], red_send.at[step])
     wait_bytes(rec_dst.at[pl.ds(0, 7)], rec_send)
@@ -316,25 +339,25 @@
     vmem = pl.BlockSpec(memory_space=pltpu.VMEM)
     final, record = pl.pallas_call(
         kernel,
-        out_shape=(jax.ShapeDtypeStruct(block, F32), jax.ShapeDtypeStruct((4, 2), F32)),
-        in_specs=[smem, smem, smem, vmem],
+        out_shape=(pltpu.VMEM(block, F32), pltpu.VMEM((2, 4), F32)),
+        in_specs=[smem, smem, smem, pl.BlockSpec(memory_space=pl.ANY)],
         out_specs=(vmem, vmem),
         scratch_shapes=[
-            pair, pair, pair, pair, pair, big, big, big, big, big,
+            big, pair, pair, pair, pair, pair, big, big, big, big, big,
             pltpu.VMEM((128, 128), F32), pltpu.VMEM((8, 8, 128), F32), pltpu.VMEM((8, 8, 128), F32),
             pltpu.VMEM((4, 2, 8, 128), F32), pltpu.VMEM((4, 2, 128), F32), pltpu.VMEM((4, 16, 2, 128), F32),
             pltpu.VMEM((8, 128), F32), pltpu.VMEM((8, 8, 128), F32),
             pltpu.SMEM((128,), F32), pltpu.SMEM((128,), F32),
             pltpu.SemaphoreType.DMA((6, SUBS)), pltpu.SemaphoreType.DMA((6, SUBS)),
             pltpu.SemaphoreType.DMA((4,)), pltpu.SemaphoreType.DMA((4,)),
-            pltpu.SemaphoreType.DMA, pltpu.SemaphoreType.DMA,
+            pltpu.SemaphoreType.DMA, pltpu.SemaphoreType.DMA, pltpu.SemaphoreType.DMA,
         ],
         compiler_params=pltpu.CompilerParams(
             collective_id=0, has_side_effects=True, vmem_limit_bytes=56 * 1024 * 1024
         ),
-    )(fields, couplings, noise.reshape(8), x)
+    )(fields, couplings, noise.transpose(0, 2, 1).reshape(2, 4), x)
     final = final.reshape(2048, 2, 128).transpose(1, 0, 2).reshape(1, 2, 262144)
-    return final, record
+    return final, record.transpose(1, 0)
 
 
 def solution(mesh):

time: 159 us -> 152 us (0.956)
  Pallas kernels: 153 us -> 149 us
  local copies, waits for them, and re-layouts: 5.28 us -> 1.88 us
    pallas_call x1, Pallas kernels: 153 us -> 149 us  [shards(): pl.pallas_call(kernel, out_shape=(pltpu.VMEM(block, F32), pltpu.VMEM((2,...]
    unnamed x3 -> x2, local copies, waits for them, and re-layouts: 4.68 us -> 1.88 us
where the time goes in v2:
time: 152 us
  Pallas kernels  149 us (98%)
  local copies, waits for them, and re-layouts  1.88 us (1%)
    pallas_call x1, Pallas kernels, shards(): pl.pallas_call(kernel, out_shape=(pltpu.VMEM(block, F32), pltpu.VMEM((2,...  149 us

profile of v2, /device:TPU:1, one launch (start us, length us, event | category | flops | bytes accessed | tf_op | source)
XLA Modules:
  0.0 152.0 jit_solution(2661385194821016146)
XLA Ops:
  0.6 149.5 %shard_map.59 = (f32[16,4,8,8,128]{4,3,2,1,0:T(8,128)S(1)}, f32[2,4]{1,0:T(2,128)S(1)}) custom-call(f32[22]{0:T(128)} %fields.1, f32[22]{0:T(128)} %couplings.1, f32[2,4]{1,0:T(2,128)} %bitcast.17, f32[16,4,8,8,128]{4,3,2,1,0:T(8,128)} %bitcast.16), custom_call_target="tpu_custom_call" | custom-call | tf_op jit(solution)/shard_map/pallas_call | solution.py:340
  150.1 1.3 copy.10
  151.5 0.6 copy.11

commit v3 on v2

v3 whole, which is shorter than its diff:
```python
import functools

import jax
import jax.numpy as jnp
from jax import lax
from jax.experimental import pallas as pl
from jax.experimental.pallas import tpu as pltpu
from jax.sharding import PartitionSpec as P

MESH = pl.DeviceIdType.MESH
KAPPA = 4.0
DT = 0.05
NQ = 22
DIM = 4194304
SUBS = 8
F32 = jnp.float32


def kernel(
    fields, couplings, noise, x_hbm, o_ref, rec_ref,
    x_ref, bp, v1b, v1a, v2b, v2a, psi1, tee, flips, why, psi2,
    table, occ_base, en_base, scal, red_src, red_dst, rec_src, rec_dst, parts, energies, pops,
    send_sem, recv_sem, red_send, red_recv, rec_send, rec_recv, load_sem,
):
    me = lax.axis_index("gx")
    gy = lax.axis_index("gy")
    n_gx, n_gy = 16, 8

    barrier = pltpu.get_barrier_semaphore()

    def greet(k, _):
        pl.semaphore_signal(barrier, inc=1, device_id=(me ^ k, gy), device_id_type=MESH)
        return 0

    def greet_y(k, _):
        pl.semaphore_signal(barrier, inc=1, device_id=(me, gy ^ k), device_id_type=MESH)
        return 0

    load = pltpu.make_async_copy(x_hbm, x_ref, load_sem)
    load.start()
    lax.fori_loop(1, n_gx, greet, 0)
    lax.fori_loop(1, n_gy, greet_y, 0)

    shape3 = (4, 8, 128)
    sub = lax.broadcasted_iota(jnp.int32, (8, 128), 0)
    lane = lax.broadcasted_iota(jnp.int32, (8, 128), 1)
    even = (sub & 1) == 0
    sign = jnp.where(even, -1.0, 1.0).astype(F32)
    bit1 = (sub & 2) == 0
    even3 = jnp.broadcast_to(even[None], shape3)
    bit1_3 = jnp.broadcast_to(bit1[None], shape3)
    z0 = 1.0 - 2.0 * (lane & 1).astype(F32)

    def times_i(y):
        return sign[None] * jnp.where(even3, pltpu.roll(y, 7, 1), pltpu.roll(y, 1, 1))

    load.wait()
    pl.semaphore_wait(barrier, n_gx - 1 + n_gy - 1)

    def partner_mask(s):
        t = s & 3
        return (1 + 2 * (t >> 1)) * (4 - 3 * (t & 1))

    def near_mask(s, i):
        t = s & 3
        return (i >> 2) * (3 - 2 * (t >> 1)) * (4 - 3 * (t & 1)) + (i & 3) * (1 + 3 * (t & 1))

    def start_copy(src, dst, move, s, other):
        pltpu.make_async_remote_copy(
            src_ref=src, dst_ref=dst, send_sem=send_sem.at[move, s], recv_sem=recv_sem.at[move, s],
            device_id=(other, gy), device_id_type=MESH,
        ).start()

    def wait_bytes(ref, sem):
        pltpu.make_async_copy(ref, ref, sem).wait()

    def wait_group(move, s, count=14):
        wait_bytes(bp.at[0, 0, pl.ds(0, count), s], recv_sem.at[move, s])

    def send_direct(src, dst, move, s):
        pm = partner_mask(s)
        partner = me ^ pm

        def one(i, _):
            other = me ^ near_mask(s, i)
            start_copy(src.at[other, s], dst.at[0, me, s], move, s, other)
            start_copy(src.at[other ^ pm, s], dst.at[1, me, s], move, s, other)
            return 0

        lax.fori_loop(1, 8, one, 0)
        start_copy(src.at[partner, s], dst.at[0, me, s], move + 1, s, partner)
        start_copy(src.at[me, s], dst.at[1, me, s], move + 1, s, partner)

    def relay(held, move, s):
        partner = me ^ partner_mask(s)

        def one(i, _):
            source = me ^ near_mask(s, i)
            start_copy(held.at[0, source, s], held.at[1, source, s], move + 1, s, partner)
            start_copy(held.at[1, source, s], held.at[0, source, s], move + 1, s, partner)
            return 0

        lax.fori_loop(1, 8, one, 0)

    def send_back(src, dst, move, s):
        pm = partner_mask(s)

        def one(i, _):
            other = me ^ near_mask(s, i)
            start_copy(src.at[0, other, s], dst.at[me, s], move, s, other)
            start_copy(src.at[1, other, s], dst.at[me ^ pm, s], move, s, other)
            return 0

        lax.fori_loop(1, 8, one, 0)

    def keep_own(src, dst):
        def one(s, _):
            dst[0, me, s] = src[me, s]
            dst[1, me, s] = src[me ^ partner_mask(s), s]
            return 0

        lax.fori_loop(0, SUBS, one, 0)

    def take_own(src, dst):
        def one(s, _):
            dst[me, s] = src[0, me, s]
            dst[me ^ partner_mask(s), s] = src[1, me, s]
            return 0

        lax.fori_loop(0, SUBS, one, 0)

    def reduce_send(step, norm8, mag8):
        both = jnp.concatenate(
            [jnp.sum(norm8, axis=0, keepdims=True), jnp.sum(mag8, axis=0, keepdims=True)], axis=0
        )
        red_src[step] = both
        red_dst[step, me] = both

        def one(k, _):
            pltpu.make_async_remote_copy(
                src_ref=red_src.at[step], dst_ref=red_dst.at[step, me],
                send_sem=red_send.at[step], recv_sem=red_recv.at[step],
                device_id=(me ^ k, gy), device_id_type=MESH,
            ).start()
            return 0

        lax.fori_loop(1, n_gx, one, 0)

    def reduce_wait(step):
        wait_bytes(red_dst.at[step, pl.ds(0, 15)], red_recv.at[step])
        total = jnp.sum(jnp.sum(red_dst[step], axis=0), axis=1, keepdims=True)
        norm, mag = total[0:1], total[1:2]
        scal[step, 0] = jnp.broadcast_to(mag / norm, (8, 128))
        scal[step, 1] = jnp.broadcast_to(jnp.sqrt(float(DIM) / norm), (8, 128))

    half_root = 0.15811388300841897

    def moved(step, which, j, s, psi, flip):
        mag, phi = scal[step, 0], scal[step, 1]
        x1 = noise[0, step] * half_root
        x2 = noise[1, step] * half_root
        d = me if which == 0 else j
        z11 = 1.0 - 2.0 * (s & 1)
        z21 = (1 - 2 * ((d >> 3) & 1)).astype(F32)
        place = which * 128 + j * 8 + s
        edge = (couplings[21] * z21) * z0 + energies[place]
        off = pops[place] - mag
        turn = couplings[10] * z11
        grows, spins = [], []
        for u in range(4):
            z10 = -1.0 if u & 2 else 1.0
            shift = occ_base[u] + off
            grows.append(phi * (1.0 + shift * (2.0 * x1 - (DT * KAPPA * 0.5) * shift)))
            energy = en_base[u] + (edge + turn * z10)
            spins.append(phi * ((2.0 * x2) * shift + DT * energy))
        return jnp.stack(grows) * psi + times_i(jnp.stack(spins) * psi + (DT * phi)[None] * flip)

    def weigh(index, psi, carry):
        norm8, mag8 = carry
        weight = psi * psi
        total = jnp.sum(weight, axis=0)
        part = jnp.sum(weight * occ_base[...], axis=0)
        return norm8 + total, mag8 + part + pops[index] * total

    zero8 = jnp.zeros((8, 128), F32)

    def local_flips(src, dst, lo=0, hi=16):
        def one(k, _):
            block = src[k]
            lanes = jnp.dot(
                block.reshape(256, 128), table[...],
                precision=lax.Precision.HIGHEST, preferred_element_type=F32,
            ).reshape(SUBS, 4, 8, 128)
            for s in range(SUBS):
                here = block[s]
                total = lanes[s]
                total = total + fields[7] * jnp.where(
                    bit1_3, pltpu.roll(here, 6, 1), pltpu.roll(here, 2, 1)
                )
                total = total + fields[8] * pltpu.roll(here, 4, 1)
                for b in range(2):
                    total = total + fields[9 + b] * jnp.stack([here[u ^ (1 << b)] for u in range(4)])
                for b in range(3):
                    total = total + fields[11 + b] * block[s ^ (1 << b)]
                for b in range(4):
                    total = total + fields[14 + b] * src[k ^ (1 << b), s]
                dst[k, s] = total
            return 0

        lax.fori_loop(lo, hi, one, 0)

    def high_flip(src, side, d, s):
        total = fields[18] * src[side, d ^ 1, s]
        for b in range(1, 4):
            total = total + fields[18 + b] * src[side, d ^ (1 << b), s]
        return total

    def round_of(r, start, finish):
        base = 4 * r
        first, second = 2 * r, 2 * r + 1
        held, out1, in1, out2, in2 = bp.at[r], v1b.at[r], v1a.at[r], v2b.at[r], v2a.at[r]
        keep_own(start, held)
        for part in range(4):
            for s in range(2 * part, 2 * part + 2):
                wait_group(base, s)
                relay(held, base, s)
            local_flips(start, flips, 4 * part, 4 * part + 4)
        for s in range(SUBS):
            wait_group(base + 1, s, 16)

            def one(d, _):
                for side in range(2):
                    out1[side, d, s] = high_flip(held, side, d, s)
                return 0

            lax.fori_loop(0, 16, one, 0)
            send_back(out1, in1, base + 2, s)
        take_own(out1, in1)
        reduce_wait(first)
        for s in range(SUBS):

            def one(d, _):
                for side in range(2):
                    why[side, d, s] = moved(first, 1 + side, d, s, held[side, d, s], out1[side, d, s])
                return 0

            lax.fori_loop(0, 16, one, 0)

            def two(i, _):
                d = me ^ near_mask(s, i)
                for side in range(2):
                    out2[side, d, s] = high_flip(why, side, d, s)
                return 0

            lax.fori_loop(0, 8, two, 0)
            if s < SUBS // 2:
                send_back(out2, in2, base + 3, s)
        take_own(out2, in2)
        carry = (zero8, zero8)
        for s in range(SUBS):
            wait_group(base + 2, s)

            def one(k, carry):
                back = in1[k, s]
                new = moved(first, 0, k, s, start[k, s], flips[k, s] + back)
                psi1[k, s] = new
                tee[k, s] = new + times_i((DT * scal[first, 1])[None] * back)
                return weigh(k * 8 + s, new, carry)

            carry = lax.fori_loop(0, 16, one, carry)
        reduce_send(second, *carry)
        for s in range(SUBS // 2, SUBS):
            send_back(out2, in2, base + 3, s)
        local_flips(tee, flips)
        reduce_wait(second)
        if r == 0:
            carry = (zero8, zero8)
            for s in range(SUBS):
                wait_group(base + 3, s)

                def one(k, carry):
                    new = moved(second, 0, k, s, psi1[k, s], flips[k, s] + in2[k, s])
                    finish[k, s] = new
                    return weigh(k * 8 + s, new, carry)

                carry = lax.fori_loop(0, 16, one, carry)
                send_direct(finish, bp.at[1], 4, s)
            reduce_send(2, *carry)
        else:
            send_record()
            for s in range(SUBS):

                def one(k, _):
                    psi1[k, s] = moved(second, 0, k, s, psi1[k, s], flips[k, s])
                    return 0

                lax.fori_loop(0, 16, one, 0)
            turn = (DT * scal[second, 1])[None]
            for s in range(SUBS):
                wait_group(base + 3, s)

                def one(k, _):
                    finish[k, s] = psi1[k, s] + times_i(turn * in2[k, s])
                    return 0

                lax.fori_loop(0, 16, one, 0)

    def send_record():
        total = zero8
        for step in range(4):
            kick = jnp.where(sub == 0, noise[0, step], noise[1, step]) * half_root
            total = total + jnp.where(lane == step, (KAPPA ** 0.5 * DT) * scal[step, 0] + kick, 0.0)
        rec_src[...] = total
        rec_dst[gy] = total

        def one(k, _):
            pltpu.make_async_remote_copy(
                src_ref=rec_src, dst_ref=rec_dst.at[gy],
                send_sem=rec_send, recv_sem=rec_recv,
                device_id=(me, gy ^ k), device_id_type=MESH,
            ).start()
            return 0

        lax.fori_loop(1, n_gy, one, 0)

    for s in range(SUBS):
        send_direct(x_ref, bp.at[0], 0, s)

    rows = lax.broadcasted_iota(jnp.int32, (128, 128), 0)
    cols = lax.broadcasted_iota(jnp.int32, (128, 128), 1)
    diff = rows ^ cols
    flip_table = jnp.zeros((128, 128), F32)
    for q in range(7):
        flip_table = jnp.where(diff == 1 << q, fields[q], flip_table)
    table[...] = flip_table
    for u in range(4):
        low = lane | ((sub >> 1) << 7) | (u << 9)
        pair = low ^ (low >> 1)
        pop = jnp.zeros((8, 128), jnp.int32)
        energy = jnp.zeros((8, 128), F32)
        for q in range(11):
            pop = pop + ((low >> q) & 1)
        for q in range(10):
            energy = energy + couplings[q] * (1.0 - 2.0 * ((pair >> q) & 1).astype(F32))
        occ_base[u] = pop.astype(F32) * (1.0 / NQ)
        en_base[u] = energy

    def spin(number, bit):
        return (1 - 2 * ((number >> bit) & 1)).astype(F32)

    def fill_parts(i, _):
        pair = i ^ (i >> 1)
        parts[i] = couplings[11] * spin(pair, 0) + couplings[12] * spin(pair, 1)
        for first, at in ((14, 16), (18, 32)):
            total = couplings[first] * spin(pair, 0)
            for b in range(1, 3):
                total = total + couplings[first + b] * spin(pair, b)
            parts[at + i] = total
        count = (i & 1) + ((i >> 1) & 1) + ((i >> 2) & 1) + ((i >> 3) & 1)
        parts[48 + i] = count.astype(F32) * (1.0 / NQ)
        return 0

    lax.fori_loop(0, 16, fill_parts, 0)

    def fill(i, _):
        j, s = i >> 3, i & 7
        for which, k, d in ((0, j, me), (1, me, j), (2, me ^ partner_mask(s), j)):
            energies[which * 128 + i] = (
                parts[s] + parts[16 + k] + parts[32 + d]
                + couplings[13] * spin((s >> 2) ^ k, 0) + couplings[17] * spin((k >> 3) ^ d, 0)
            )
            pops[which * 128 + i] = parts[48 + s] + parts[48 + k] + parts[48 + d]
        return 0

    lax.fori_loop(0, 128, fill, 0)

    def first_weigh(i, carry):
        return weigh(i, x_ref[i >> 3, i & 7], carry)

    reduce_send(0, *lax.fori_loop(0, 128, first_weigh, (zero8, zero8)))
    round_of(0, x_ref, psi2)
    round_of(1, psi2, o_ref)

    wait_bytes(rec_dst.at[pl.ds(0, 7)], rec_recv)
    rec_ref[...] = jnp.sum(rec_dst[...], axis=0)[0:2, 0:4]

    for move in range(8):
        for s in range(SUBS):
            count = 16 if move % 4 == 1 else 14
            wait_bytes(bp.at[0, 0, pl.ds(0, count), s], send_sem.at[move, s])
    for step in range(4):
        wait_bytes(red_dst.at[step, pl.ds(0, 15)], red_send.at[step])
    wait_bytes(rec_dst.at[pl.ds(0, 7)], rec_send)


def shards(state, fields, couplings, noise):
    block = (16, SUBS, 4, 8, 128)
    x = state.reshape(2, 2048, 128).transpose(1, 0, 2).reshape(block)
    big = pltpu.VMEM(block, F32)
    pair = pltpu.VMEM((2, *block), F32)
    twin = pltpu.VMEM((2, 2, *block), F32)
    smem = pl.BlockSpec(memory_space=pltpu.SMEM)
    vmem = pl.BlockSpec(memory_space=pltpu.VMEM)
    final, record = pl.pallas_call(
        kernel,
        out_shape=(pltpu.VMEM(block, F32), pltpu.VMEM((2, 4), F32)),
        in_specs=[smem, smem, smem, pl.BlockSpec(memory_space=pl.ANY)],
        out_specs=(vmem, vmem),
        scratch_shapes=[
            big, twin, twin, pair, twin, pair, big, big, big, pair, big,
            pltpu.VMEM((128, 128), F32), pltpu.VMEM((4, 8, 128), F32), pltpu.VMEM((4, 8, 128), F32),
            pltpu.VMEM((4, 2, 8, 128), F32), pltpu.VMEM((4, 2, 128), F32), pltpu.VMEM((4, 16, 2, 128), F32),
            pltpu.VMEM((8, 128), F32), pltpu.VMEM((8, 8, 128), F32),
            pltpu.SMEM((64,), F32), pltpu.SMEM((384,), F32), pltpu.SMEM((384,), F32),
            pltpu.SemaphoreType.DMA((8, SUBS)), pltpu.SemaphoreType.DMA((8, SUBS)),
            pltpu.SemaphoreType.DMA((4,)), pltpu.SemaphoreType.DMA((4,)),
            pltpu.SemaphoreType.DMA, pltpu.SemaphoreType.DMA, pltpu.SemaphoreType.DMA,
        ],
        compiler_params=pltpu.CompilerParams(
            collective_id=0, has_side_effects=True, vmem_limit_bytes=60 * 1024 * 1024
        ),
    )(fields, couplings, noise.transpose(0, 2, 1).reshape(2, 4), x)
    final = final.reshape(2048, 2, 128).transpose(1, 0, 2).reshape(1, 2, 262144)
    return final, record.transpose(1, 0)


def solution(mesh):
    placed = (P("gy", None, "gx"), P(), P(), P("gy", None, None))
    return jax.shard_map(
        shards, mesh=mesh, in_specs=placed, out_specs=(P("gy", None, "gx"), P()), check_vma=False
    )
```

time: 152 us -> 138 us (0.908)
  Pallas kernels: 149 us -> 136 us
    pallas_call x1, Pallas kernels: 149 us -> 136 us  [shards(): pl.pallas_call(kernel, out_shape=(pltpu.VMEM(block, F32), pltpu.VMEM((2,...]
where the time goes in v3:
time: 138 us
  Pallas kernels  136 us (99%)
  local copies, waits for them, and re-layouts  1.88 us (1%)
    pallas_call x1, Pallas kernels, shards(): pl.pallas_call(kernel, out_shape=(pltpu.VMEM(block, F32), pltpu.VMEM((2,...  136 us

profile of v3, /device:TPU:1, one launch (start us, length us, event | category | flops | bytes accessed | tf_op | source)
XLA Modules:
  0.0 138.3 jit_solution(15826861651256427059)
XLA Ops:
  0.6 135.8 %shard_map.59 = (f32[16,8,4,8,128]{4,3,2,1,0:T(8,128)S(1)}, f32[2,4]{1,0:T(2,128)S(1)}) custom-call(f32[22]{0:T(128)} %fields.1, f32[22]{0:T(128)} %couplings.1, f32[2,4]{1,0:T(2,128)} %bitcast.17, f32[16,8,4,8,128]{4,3,2,1,0:T(8,128)} %bitcast.16), custom_call_target="tpu_custom_call" | custom-call | tf_op jit(solution)/shard_map/pallas_call | solution.py:404
  136.4 1.3 copy.10
  137.8 0.6 copy.11

commit v4 on v3

--- a/solution.py
+++ b/solution.py
@@ -295,6 +295,7 @@
                     return 0
 
                 lax.fori_loop(0, 16, one, 0)
+            settle()
             turn = (DT * scal[second, 1])[None]
             for s in range(SUBS):
                 wait_group(base + 3, s)
@@ -322,6 +323,20 @@
             return 0
 
         lax.fori_loop(1, n_gy, one, 0)
+
+    def wait_sent(move):
+        for s in range(SUBS):
+            count = 16 if move % 4 == 1 else 14
+            wait_bytes(bp.at[0, 0, pl.ds(0, count), s], send_sem.at[move, s])
+
+    def settle():
+        wait_bytes(rec_dst.at[pl.ds(0, 7)], rec_recv)
+        rec_ref[...] = jnp.sum(rec_dst[...], axis=0)[0:2, 0:4]
+        for move in range(7):
+            wait_sent(move)
+        for step in range(4):
+            wait_bytes(red_dst.at[step, pl.ds(0, 15)], red_send.at[step])
+        wait_bytes(rec_dst.at[pl.ds(0, 7)], rec_send)
 
     for s in range(SUBS):
         send_direct(x_ref, bp.at[0], 0, s)
@@ -381,16 +396,16 @@
     round_of(0, x_ref, psi2)
     round_of(1, psi2, o_ref)
 
-    wait_bytes(rec_dst.at[pl.ds(0, 7)], rec_recv)
-    rec_ref[...] = jnp.sum(rec_dst[...], axis=0)[0:2, 0:4]
-
-    for move in range(8):
-        for s in range(SUBS):
-            count = 16 if move % 4 == 1 else 14
-            wait_bytes(bp.at[0, 0, pl.ds(0, count), s], send_sem.at[move, s])
-    for step in range(4):
-        wait_bytes(red_dst.at[step, pl.ds(0, 15)], red_send.at[step])
-    wait_bytes(rec_dst.at[pl.ds(0, 7)], rec_send)
+    wait_sent(7)
+
+
+def store(final, record, final_hbm, record_hbm, sems):
+    first = pltpu.make_async_copy(final, final_hbm, sems.at[0])
+    second = pltpu.make_async_copy(record, record_hbm, sems.at[1])
+    first.start()
+    second.start()
+    second.wait()
+    first.wait()
 
 
 def shards(state, fields, couplings, noise):
@@ -420,6 +435,15 @@
             collective_id=0, has_side_effects=True, vmem_limit_bytes=60 * 1024 * 1024
         ),
     )(fields, couplings, noise.transpose(0, 2, 1).reshape(2, 4), x)
+    hbm = pl.BlockSpec(memory_space=pl.ANY)
+    final, record = pl.pallas_call(
+        store,
+        out_shape=(jax.ShapeDtypeStruct(block, F32), jax.ShapeDtypeStruct((2, 4), F32)),
+        in_specs=[vmem, vmem],
+        out_specs=(hbm, hbm),
+        scratch_shapes=[pltpu.SemaphoreType.DMA((2,))],
+        compiler_params=pltpu.CompilerParams(vmem_limit_bytes=256 * 1024),
+    )(final, record)
     final = final.reshape(2048, 2, 128).transpose(1, 0, 2).reshape(1, 2, 262144)
     return final, record.transpose(1, 0)
 

time: 138 us -> 138 us (level)
  local copies, waits for them, and re-layouts: 1.88 us -> 0 us
    unnamed x2 -> x0, local copies, waits for them, and re-layouts: 1.88 us -> none
where the time goes in v4:
time: 138 us
  Pallas kernels  137 us (99%)
    pallas_call x1, Pallas kernels, shards(): pl.pallas_call(kernel, out_shape=(pltpu.VMEM(block, F32), pltpu.VMEM((2,...  136 us

profile of v4, /device:TPU:1, one launch (start us, length us, event | category | flops | bytes accessed | tf_op | source)
XLA Modules:
  0.0 137.7 jit_solution(7768645158190089888)
XLA Ops:
  0.6 135.7 %shard_map.59 = (f32[16,8,4,8,128]{4,3,2,1,0:T(8,128)S(1)}, f32[2,4]{1,0:T(2,128)S(1)}) custom-call(f32[22]{0:T(128)} %fields.1, f32[22]{0:T(128)} %couplings.1, f32[2,4]{1,0:T(2,128)} %bitcast.15, f32[16,8,4,8,128]{4,3,2,1,0:T(8,128)} %bitcast.14), custom_call_target="tpu_custom_call" | custom-call | tf_op jit(solution)/shard_map/pallas_call | solution.py:419
  136.3 1.3 shard_map.60

commit v5 on v4

--- a/solution.py
+++ b/solution.py
@@ -130,9 +130,9 @@
         lax.fori_loop(0, SUBS, one, 0)
 
     def reduce_send(step, norm8, mag8):
-        both = jnp.concatenate(
-            [jnp.sum(norm8, axis=0, keepdims=True), jnp.sum(mag8, axis=0, keepdims=True)], axis=0
-        )
+        norm = jnp.sum(norm8, axis=0, keepdims=True)
+        mag = jnp.sum(mag8, axis=0, keepdims=True)
+        both = jnp.where(lane[0:1] < 64, norm + pltpu.roll(norm, 64, 1), mag + pltpu.roll(mag, 64, 1))
         red_src[step] = both
         red_dst[step, me] = both
 
@@ -148,8 +148,10 @@
 
     def reduce_wait(step):
         wait_bytes(red_dst.at[step, pl.ds(0, 15)], red_recv.at[step])
-        total = jnp.sum(jnp.sum(red_dst[step], axis=0), axis=1, keepdims=True)
-        norm, mag = total[0:1], total[1:2]
+        total = jnp.sum(red_dst[step], axis=0)
+        low = lane[0:1] < 64
+        norm = jnp.sum(jnp.where(low, total, 0.0), axis=1, keepdims=True)
+        mag = jnp.sum(jnp.where(low, 0.0, total), axis=1, keepdims=True)
         scal[step, 0] = jnp.broadcast_to(mag / norm, (8, 128))
         scal[step, 1] = jnp.broadcast_to(jnp.sqrt(float(DIM) / norm), (8, 128))
 
@@ -400,12 +402,14 @@
 
 
 def store(final, record, final_hbm, record_hbm, sems):
-    first = pltpu.make_async_copy(final, final_hbm, sems.at[0])
-    second = pltpu.make_async_copy(record, record_hbm, sems.at[1])
-    first.start()
-    second.start()
-    second.wait()
-    first.wait()
+    copies = [pltpu.make_async_copy(record, record_hbm, sems.at[0])]
+    for i in range(4):
+        rows = pl.ds(4 * i, 4)
+        copies.append(pltpu.make_async_copy(final.at[rows], final_hbm.at[rows], sems.at[1 + i]))
+    for copy in copies:
+        copy.start()
+    for copy in copies:
+        copy.wait()
 
 
 def shards(state, fields, couplings, noise):
@@ -424,7 +428,7 @@
         scratch_shapes=[
             big, twin, twin, pair, twin, pair, big, big, big, pair, big,
             pltpu.VMEM((128, 128), F32), pltpu.VMEM((4, 8, 128), F32), pltpu.VMEM((4, 8, 128), F32),
-            pltpu.VMEM((4, 2, 8, 128), F32), pltpu.VMEM((4, 2, 128), F32), pltpu.VMEM((4, 16, 2, 128), F32),
+            pltpu.VMEM((4, 2, 8, 128), F32), pltpu.VMEM((4, 1, 128), F32), pltpu.VMEM((4, 16, 1, 128), F32),
             pltpu.VMEM((8, 128), F32), pltpu.VMEM((8, 8, 128), F32),
             pltpu.SMEM((64,), F32), pltpu.SMEM((384,), F32), pltpu.SMEM((384,), F32),
             pltpu.SemaphoreType.DMA((8, SUBS)), pltpu.SemaphoreType.DMA((8, SUBS)),
@@ -441,7 +445,7 @@
         out_shape=(jax.ShapeDtypeStruct(block, F32), jax.ShapeDtypeStruct((2, 4), F32)),
         in_specs=[vmem, vmem],
         out_specs=(hbm, hbm),
-        scratch_shapes=[pltpu.SemaphoreType.DMA((2,))],
+        scratch_shapes=[pltpu.SemaphoreType.DMA((5,))],
         compiler_params=pltpu.CompilerParams(vmem_limit_bytes=256 * 1024),
     )(final, record)
     final = final.reshape(2048, 2, 128).transpose(1, 0, 2).reshape(1, 2, 262144)

time: 138 us -> 138 us (level)
  no operation moved by 1% of the time
where the time goes in v5:
time: 138 us; the launch traced here: 137 us
  Pallas kernels  137 us (99%)
    pallas_call x1, Pallas kernels, shards(): pl.pallas_call(kernel, out_shape=(pltpu.VMEM(block, F32), pltpu.VMEM((2,...  135 us

profile of v5, /device:TPU:1, one launch (start us, length us, event | category | flops | bytes accessed | tf_op | source)
XLA Modules:
  0.0 137.3 jit_solution(16183345628175212015)
XLA Ops:
  0.6 135.3 %shard_map.59 = (f32[16,8,4,8,128]{4,3,2,1,0:T(8,128)S(1)}, f32[2,4]{1,0:T(2,128)S(1)}) custom-call(f32[22]{0:T(128)} %fields.1, f32[22]{0:T(128)} %couplings.1, f32[2,4]{1,0:T(2,128)} %bitcast.15, f32[16,8,4,8,128]{4,3,2,1,0:T(8,128)} %bitcast.14), custom_call_target="tpu_custom_call" | custom-call | tf_op jit(solution)/shard_map/pallas_call | solution.py:423
  136.0 1.4 shard_map.60
